TPU v7x, 32 devices: a whole 2x2x4 slice. The times are simulated.
32 devices in a mesh: dp: 16 (over z, x, core), tensor: 2 (over y).
Axes of the slice: x: 2, y: 2, z: 4, core: 2. Of those that a mesh axis runs over, the one named last changes fastest.
Arguments:
- query_rows: bfloat16 [6144, 5120], P('dp', 'tensor'), may hold values from -128 to 128
- key_rows: bfloat16 [6144, 5120], P('dp', 'tensor'), may hold values from -5 to 5
- value_rows: bfloat16 [6144, 5120], P('dp', 'tensor'), may hold values from -12 to 12
- action_mask: int32 [16, 384], P('dp'), may hold values from 0 to 1, as said below
- residual: bfloat16 [6144, 5120], P('dp', 'tensor'), may hold values from -100 to 100
- out_weight: bfloat16 [5120, 5120], P(None, 'tensor'), may hold values from -0.078125 to 0.078125
- norm_gain: float32 [5120], P('tensor'), may hold values from 0.1 to 1.9
- upstream: bfloat16 [6144, 5120], P('dp', 'tensor'), may hold values from -6 to 6
- residual_grad: bfloat16 [6144, 5120], P('dp', 'tensor'), may hold values from -2 to 2
Outputs:
- layer_out: bfloat16 [6144, 5120], P('dp', 'tensor')
- grad_residual: bfloat16 [6144, 5120], P('dp', 'tensor')
- grad_query: bfloat16 [6144, 5120], P('dp', 'tensor')
- grad_key: bfloat16 [6144, 5120], P('dp', 'tensor')
- grad_value: bfloat16 [6144, 5120], P('dp', 'tensor')
- grad_out_weight: float32 [5120, 5120], P('dp', 'tensor')
- grad_gain: float32 [5120], P('tensor')
Inputs may be any that keep to these rules, and one draw needn't show every extreme that they name: `action_mask`: each row is a run of zeros followed by a run of ones; the ones number 1 to 192.
All inputs are finite; a program needn't handle non-finite values.
Results may differ from a plain program's by a relative error of at most 0.015.
Values may be sent and summed in bfloat16 or wider, within the bound.
A program may use at most 192 MiB of HBM per device.

v0:
```python
import jax
import jax.numpy as jnp
from jax import lax
from jax.sharding import PartitionSpec as P

D = 5120
HEAD_DIM = 128
LEN = 384
epsilon = 1e-05


def visible(mask_row):
    position = jnp.arange(mask_row.shape[0])
    causal = position[None, :] <= position[:, None]
    observe = mask_row == 0
    return causal | observe[:, None] & observe[None, :]


def shards(
    query_rows,
    key_rows,
    value_rows,
    action_mask,
    residual,
    out_weight,
    norm_gain,
    upstream,
    residual_grad,
):
    seq_count = action_mask.shape[0]
    tok_rows = query_rows.shape[0]
    local_width = query_rows.shape[1]
    head_shape = (seq_count, LEN, local_width // HEAD_DIM, HEAD_DIM)
    query_heads = query_rows.reshape(head_shape)
    key_heads = key_rows.reshape(head_shape)
    value_heads = value_rows.reshape(head_shape)
    score_scale = HEAD_DIM ** (-0.5)
    allowed = jax.vmap(visible)(action_mask)
    scores = (
        jnp.einsum("sqhd,skhd->shqk", query_heads, key_heads, preferred_element_type=jnp.float32)
        * score_scale
    )
    masked = jnp.where(allowed[:, None], scores, -jnp.inf)
    row_top = jnp.max(masked, axis=-1, keepdims=True)
    weights = jnp.exp(masked - row_top)
    chances = weights / jnp.sum(weights, axis=-1, keepdims=True)
    chances_low = chances.astype(jnp.bfloat16)
    attended = jnp.einsum(
        "shqk,skhd->sqhd", chances_low, value_heads, preferred_element_type=jnp.float32
    )
    attended = attended.astype(jnp.bfloat16).reshape(tok_rows, local_width)
    projected = jnp.dot(attended, out_weight.T, preferred_element_type=jnp.float32)
    own_width = residual.shape[1]
    full_sum = lax.psum(projected, "tensor")
    own_sum = lax.dynamic_slice_in_dim(full_sum, lax.axis_index("tensor") * own_width, own_width, 1)
    layer_out = (own_sum + residual.astype(jnp.float32)).astype(jnp.bfloat16)
    out_float = layer_out.astype(jnp.float32)
    upstream_float = upstream.astype(jnp.float32)
    scaled = upstream_float * norm_gain[None, :]
    square_sum, inner_sum = lax.psum(
        (jnp.sum(out_float * out_float, axis=1), jnp.sum(scaled * out_float, axis=1)), "tensor"
    )
    row_rms = jnp.sqrt(square_sum / D + epsilon)[:, None]
    normed = out_float / row_rms
    row_inner = inner_sum[:, None] / (row_rms * D)
    grad_residual = (
        residual_grad.astype(jnp.float32) + (scaled - normed * row_inner) / row_rms
    ).astype(jnp.bfloat16)
    grad_gain = lax.psum(jnp.sum(upstream_float * normed, axis=0), "dp")
    grad_full = lax.all_gather(grad_residual, "tensor", axis=1, tiled=True)
    grad_attended = jnp.dot(grad_full, out_weight, preferred_element_type=jnp.float32).astype(
        jnp.bfloat16
    )
    contract_rows = (((0,), (0,)), ((), ()))
    received = lax.all_to_all(grad_full, "dp", split_axis=1, concat_axis=0, tiled=True)
    grad_out_weight = lax.dot_general(
        received,
        lax.all_gather(attended, "dp", axis=0, tiled=True),
        contract_rows,
        preferred_element_type=jnp.float32,
    )
    grad_heads = grad_attended.reshape(head_shape)
    grad_value = jnp.einsum(
        "shqk,sqhd->skhd", chances_low, grad_heads, preferred_element_type=jnp.float32
    ).astype(jnp.bfloat16)
    grad_chances = jnp.einsum(
        "sqhd,skhd->shqk", grad_heads, value_heads, preferred_element_type=jnp.float32
    )
    row_delta = jnp.sum(chances * grad_chances, axis=-1, keepdims=True)
    grad_scores = (chances * (grad_chances - row_delta) * score_scale).astype(jnp.bfloat16)
    grad_query = jnp.einsum(
        "shqk,skhd->sqhd", grad_scores, key_heads, preferred_element_type=jnp.float32
    ).astype(jnp.bfloat16)
    grad_key = jnp.einsum(
        "shqk,sqhd->skhd", grad_scores, query_heads, preferred_element_type=jnp.float32
    ).astype(jnp.bfloat16)
    return (
        layer_out,
        grad_residual,
        grad_query.reshape(tok_rows, local_width),
        grad_key.reshape(tok_rows, local_width),
        grad_value.reshape(tok_rows, local_width),
        grad_out_weight,
        grad_gain,
    )


def solution(mesh):
    placed = (
        P("dp", "tensor"),
        P("dp", "tensor"),
        P("dp", "tensor"),
        P("dp", None),
        P("dp", "tensor"),
        P(None, "tensor"),
        P("tensor"),
        P("dp", "tensor"),
        P("dp", "tensor"),
    )
    return jax.shard_map(
        shards,
        mesh=mesh,
        in_specs=placed,
        out_specs=(
            P("dp", "tensor"),
            P("dp", "tensor"),
            P("dp", "tensor"),
            P("dp", "tensor"),
            P("dp", "tensor"),
            P("dp", "tensor"),
            P("tensor"),
        ),
        check_vma=False,
    )
```

profile of v0, /device:TPU:0, one launch (start us, length us, event | category | flops | bytes accessed | tf_op | source)
XLA Modules:
  0.0 635.0 jit_solution(9114788977476758334)
XLA Ops:
  7.2 0.0 copy-start.6
  7.2 0.0 all-reduce.2.cloned.1.call-start
  7.2 2.8 copy.35
  10.1 0.0 copy-done.6
  10.1 0.0 copy-start.1
  10.1 0.1 fusion.40
  10.3 4.4 copy.31
  14.7 3.9 copy.32
  18.6 10.4 %fusion.47 = (f32[20,384]{1,0:T(8,128)S(1)}, f32[20,384,384]{1,2,0:T(8,128)}) fusion(pred[384,384]{0,1:T(8,128)(4,1)S(1)} %fusion.40, bf16[384,20,128]{0,2,1:T(8,128)(2,1)} %bitcast.58, bf16[384,20,128]{0,2,1:T(8,128)(2,1)} %bitcast.60), kind=kOutput, calls=%fused_computation.48 | convolution fusion | flops 766771584 | bytes 15906816 | tf_op jit(solution)/shard_map/sub | solution.py:45
  29.0 0.0 copy-done.1
  29.0 7.1 %fusion.26 = bf16[20,384,128]{1,2,0:T(8,128)(2,1)} fusion(bf16[384,20,128]{0,2,1:T(8,128)(2,1)S(1)} %bitcast.51, f32[20,384,384]{1,2,0:T(8,128)} %get-tuple-element.26, f32[20,384]{1,0:T(8,128)S(1)} %get-tuple-element.25), kind=kOutput, calls=%fused_computation.32 | convolution fusion | flops 761856000 | bytes 15759360 | tf_op jit(solution)/shard_map/shqk,skhd->sqhd/dot_general | solution.py:48
  36.1 17.8 %fusion.48 = f32[384,5120]{1,0:T(8,128)} fusion(bf16[384,2560]{0,1:T(8,128)(2,1)} %bitcast.56, bf16[5120,2560]{1,0:T(8,128)(2,1)} %param.14), kind=kOutput, calls=%fused_computation.49 | convolution fusion | flops 10066329600 | bytes 36044800 | tf_op jit(solution)/shard_map/dot_general | solution.py:52
  53.9 0.0 all-reduce.2.cloned.1.call-update
  54.0 0.2 all-gather.3.cloned.1.call-start
  54.2 0.0 copy-start.5
  54.2 189.9 %all-reduce.2.cloned.1.call-done = f32[384,5120]{1,0:T(8,128)} async-done(((f32[384,5120]{1,0:T(8,128)}), f32[384,5120]{1,0:T(8,128)}) %all-reduce.2.cloned.1.call-update) | async-done | bytes 7864336 | tf_op jit(solution)/shard_map/psum | solution.py:54
  244.1 3.4 fusion.19
  247.5 0.0 copy-start
  247.5 4.9 psum.29
  252.5 0.0 copy-done.5
  252.5 3.1 fusion.18
  255.5 4.9 psum.30
  260.5 5.0 fusion.21
  265.4 0.0 copy-done
  265.4 0.0 all-gather.3.cloned.1.call-update
  265.5 0.0 all-gather.5.cloned.1.call-start
  265.5 0.7 all-gather.5.cloned.1.call-update
  266.2 53.2 %all-gather.3.cloned.1.call-done = bf16[384,5120]{1,0:T(8,128)(2,1)} async-done(((bf16[384,2560]{1,0:T(8,128)(2,1)}), bf16[384,5120]{1,0:T(8,128)(2,1)}) %all-gather.3.cloned.1.call-update) | async-done | bytes 3932176 | tf_op jit(solution)/shard_map/all_gather | solution.py:70
  319.4 6.3 copy.43
  325.7 5.7 all-to-all-start
  331.3 185.8 %psum.31 = f32[2560]{0:T(1024)} all-reduce(f32[2560]{0:T(1024)S(1)} %get-tuple-element.21), channel_id=1, replica_groups=mesh['dp'=16,'tensor'=2] {'dp'}, use_global_device_ids=true, to_apply=%region_9.10 | all-reduce | flops 2560 | bytes 20480 | tf_op jit(solution)/shard_map/psum | solution.py:69
  517.1 17.4 %convolution_convert_fusion = bf16[384,2560]{1,0:T(8,128)(2,1)} fusion(bf16[384,5120]{1,0:T(8,128)(2,1)} %all-gather.3.cloned.1.call-done, bf16[5120,2560]{1,0:T(8,128)(2,1)} %param.14), kind=kOutput, calls=%fused_computation.20 | convolution fusion | flops 10067312640 | bytes 32112640 | tf_op jit(solution)/shard_map/dot_general | solution.py:71
  534.5 0.0 copy-start.2
  534.5 4.2 copy.37
  538.7 0.0 copy-done.2
  538.7 7.6 %fusion.49 = f32[20,384,384]{1,2,0:T(8,128)} fusion(bf16[384,20,128]{0,2,1:T(8,128)(2,1)} %bitcast.53, bf16[384,20,128]{0,2,1:T(8,128)(2,1)S(1)} %bitcast.52), kind=kOutput, calls=%fused_computation.50 | convolution fusion | flops 754974720 | bytes 15728640 | tf_op jit(solution)/shard_map/sqhd,skhd->shqk/dot_general | solution.py:86
  546.3 20.3 %fusion.32 = bf16[20,384,128]{1,2,0:T(8,128)(2,1)} fusion(bf16[384,20,128]{0,2,1:T(8,128)(2,1)} %bitcast.61, f32[20,384,384]{1,2,0:T(8,128)} %fusion.49, f32[20,384,384]{1,2,0:T(8,128)} %get-tuple-element.26, f32[20,384]{1,0:T(8,128)S(1)} %get-tuple-element.25), kind=kOutput, calls=%fused_computation.34 | convolution fusion | flops 776609664 | bytes 27555840 | tf_op jit(solution)/shard_map/shqk,skhd->sqhd/dot_general | solution.py:91
  566.6 0.0 copy-start.4
  566.6 4.1 copy.45
  570.7 0.0 copy-done.4
  570.7 19.7 %fusion.35 = bf16[20,384,128]{1,2,0:T(8,128)(2,1)} fusion(bf16[384,20,128]{0,2,1:T(8,128)(2,1)S(1)} %bitcast.59, f32[20,384,384]{1,2,0:T(8,128)} %fusion.49, f32[20,384,384]{1,2,0:T(8,128)} %get-tuple-element.26, f32[20,384]{1,0:T(8,128)S(1)} %get-tuple-element.25), kind=kOutput, calls=%fused_computation.35 | convolution fusion | flops 776609664 | bytes 27555840 | tf_op jit(solution)/shard_map/shqk,sqhd->skhd/dot_general | solution.py:94
  590.4 0.0 copy-start.3
  590.5 4.1 copy.46
  594.6 0.0 copy-done.3
  594.6 7.5 %fusion.29 = bf16[20,128,384]{2,1,0:T(8,128)(2,1)} fusion(bf16[384,20,128]{0,2,1:T(8,128)(2,1)S(1)} %bitcast.54, f32[20,384,384]{1,2,0:T(8,128)} %get-tuple-element.26, f32[20,384]{1,0:T(8,128)S(1)} %get-tuple-element.25), kind=kOutput, calls=%fused_computation.33 | convolution fusion | flops 761856000 | bytes 15759360 | tf_op jit(solution)/shard_map/shqk,sqhd->skhd/dot_general | solution.py:83
  602.1 4.0 copy.47
  606.1 0.0 all-to-all-done
  606.1 4.7 copy.56
  610.8 0.0 all-gather.5.cloned.1.call-done
  610.8 17.7 %fusion.50 = f32[320,2560]{1,0:T(8,128)} fusion(bf16[6144,320]{0,1:T(8,128)(2,1)} %bitcast.55, bf16[6144,2560]{0,1:T(8,128)(2,1)} %all-gather.5.cloned.1.call-done), kind=kOutput, calls=%fused_computation.51 | convolution fusion | flops 10066329600 | bytes 38666240 | tf_op jit(solution)/shard_map/dot_general | solution.py:76
  (3 shorter events, 0.0 us)
Async XLA Ops:
  7.2 2.9 copy-start.6
  7.2 236.9 %all-reduce.2.cloned.1.call-start = ((), (), s32[]{:S(2)}) async-start(), calls=%async_computation.1 | async-start | bytes 15728640 | tf_op jit(solution)/shard_map/psum | solution.py:54
  10.1 18.9 %copy-start.1 = (bf16[384,2560]{0,1:T(8,128)(2,1)}, bf16[384,2560]{0,1:T(8,128)(2,1)S(1)}, u32[]{:S(2)}) copy-start(bf16[384,2560]{0,1:T(8,128)(2,1)S(1)} %copy.35) | copy-start | bytes 5898244
  54.0 265.4 %all-gather.3.cloned.1.call-start = ((), (), s32[]{:S(2)}) async-start(), calls=%async_computation.2 | async-start | bytes 5898240 | tf_op jit(solution)/shard_map/all_gather | solution.py:70
  54.2 198.3 %copy-start.5 = (f32[2560]{0:T(1024)S(1)}, f32[2560]{0:T(1024)}, u32[]{:S(2)}) copy-start(f32[2560]{0:T(1024)} %param.15) | copy-start | bytes 30724
  247.5 17.9 %copy-start = (bf16[384,2560]{1,0:T(8,128)(2,1)}, bf16[384,2560]{1,0:T(8,128)(2,1)S(1)}, u32[]{:S(2)}) copy-start(bf16[384,2560]{1,0:T(8,128)(2,1)S(1)} %get-tuple-element.24) | copy-start | bytes 5898244
  265.5 345.3 %all-gather.5.cloned.1.call-start = ((), (), s32[]{:S(2)}) async-start(), calls=%async_computation.3 | async-start | bytes 33423360 | tf_op jit(solution)/shard_map/all_gather | solution.py:78
  325.7 280.4 %all-to-all-start = ((bf16[384,16,320]{0,2,1:T(8,128)(2,1)}), bf16[384,16,320]{0,2,1:T(8,128)(2,1)}, u32[]{:S(2)}, u32[]{:S(2)}) async-start(bf16[384,16,320]{0,2,1:T(8,128)(2,1)} %bitcast.50), calls=%async_computation | async-start | bytes 7864320 | tf_op jit(solution)/shard_map/all_to_all | solution.py:75
  534.5 4.2 copy-start.2
  566.6 4.1 copy-start.4
  590.4 4.1 copy-start.3
Sparse Core Ops, SparseCore 0:
  54.1 189.9 all-reduce.1
  265.6 53.7 all-gather.2
  321.5 231.1 all-gather.4
where the time goes:
time: 636 us; the launch traced here: 635 us
  waiting for transfers between devices  244 us (38%)
  blocking collectives  196 us (31%)
  matrix products  126 us (20%)
  local copies, waits for them, and re-layouts  38.5 us (6%)
  between operations  13.8 us (2%)
  other arithmetic  11.7 us (2%)
    psum x1, waiting for transfers between devices, shards(): full_sum = lax.psum(projected, 'tensor')  190 us
    psum x1, blocking collectives, shards(): grad_gain = lax.psum(jnp.sum(upstream_float * normed, axis=0), 'dp')  186 us
    all_gather x1, waiting for transfers between devices, shards(): grad_full = lax.all_gather(grad_residual, 'tensor', axis=1, tiled=True)  53.2 us
    unnamed x20, local copies, waits for them, and re-layouts  23.4 us
    dot_general x1, matrix products, shards(): jnp.einsum('shqk,skhd->sqhd', grad_scores, key_heads, preferred_element_t...  20.3 us
    dot_general x1, matrix products, shards(): jnp.einsum('shqk,sqhd->skhd', grad_scores, query_heads, preferred_element...  19.7 us
    dot_general x1, matrix products, shards(): jnp.dot(attended, out_weight.T, preferred_element_type=jnp.float32)  17.8 us
    dot_general x1, matrix products, shards(): lax.dot_general(received, lax.all_gather(attended, 'dp', axis=0, tiled=Tr...  17.7 us
  transfers between devices with their start and end apart: 4, of which 2 were waited for; matrix products, arithmetic and copies ran while one was open for 16% of the time, Pallas kernels for 0%

commit v1 on v0

--- a/solution.py
+++ b/solution.py
@@ -66,7 +66,9 @@
     grad_residual = (
         residual_grad.astype(jnp.float32) + (scaled - normed * row_inner) / row_rms
     ).astype(jnp.bfloat16)
-    grad_gain = lax.psum(jnp.sum(upstream_float * normed, axis=0), "dp")
+    x = jnp.sum(upstream_float * normed, axis=0)
+    parts = lax.all_gather(x, "dp")
+    grad_gain = jnp.sum(parts, axis=0)
     grad_full = lax.all_gather(grad_residual, "tensor", axis=1, tiled=True)
     grad_attended = jnp.dot(grad_full, out_weight, preferred_element_type=jnp.float32).astype(
         jnp.bfloat16

time: 636 us -> 595 us (0.936)
  blocking collectives: 196 us -> 154 us
    psum x1 -> x0, blocking collectives: 186 us -> none  [shards(): grad_gain = lax.psum(jnp.sum(upstream_float * normed, axis=0), 'dp')]
    all_gather x0 -> x1, blocking collectives: none -> 144 us  [shards(): parts = lax.all_gather(x, 'dp')]
    unnamed x20 -> x21, local copies, waits for them, and re-layouts: 23.4 us -> 23.5 us
  transfers between devices with their start and end apart: 4 -> 4, of which waited for: 2 -> 2; matrix products, arithmetic and copies ran while one was open for 16% -> 17% of each run, Pallas kernels for 0% -> 0%
where the time goes in v1:
time: 595 us; the launch traced here: 594 us
  waiting for transfers between devices  244 us (41%)
  blocking collectives  154 us (26%)
  matrix products  126 us (21%)
  local copies, waits for them, and re-layouts  38.6 us (6%)
  between operations  13.8 us (2%)
  other arithmetic  12.4 us (2%)
  starting transfers between devices  5.96 us (1%)
    psum x1, waiting for transfers between devices, shards(): full_sum = lax.psum(projected, 'tensor')  190 us
    all_gather x1, blocking collectives, shards(): parts = lax.all_gather(x, 'dp')  144 us
    all_gather x1, waiting for transfers between devices, shards(): grad_full = lax.all_gather(grad_residual, 'tensor', axis=1, tiled=True)  53.2 us
    unnamed x21, local copies, waits for them, and re-layouts  23.5 us
    dot_general x1, matrix products, shards(): jnp.einsum('shqk,skhd->sqhd', grad_scores, key_heads, preferred_element_t...  20.3 us
    dot_general x1, matrix products, shards(): jnp.einsum('shqk,sqhd->skhd', grad_scores, query_heads, preferred_element...  19.7 us
    dot_general x1, matrix products, shards(): jnp.dot(attended, out_weight.T, preferred_element_type=jnp.float32)  17.8 us
    dot_general x1, matrix products, shards(): lax.dot_general(received, lax.all_gather(attended, 'dp', axis=0, tiled=Tr...  17.7 us
  transfers between devices with their start and end apart: 4, of which 2 were waited for; matrix products, arithmetic and copies ran while one was open for 17% of the time, Pallas kernels for 0%

profile of v1, /device:TPU:0, one launch (start us, length us, event | category | flops | bytes accessed | tf_op | source)
XLA Modules:
  0.0 593.6 jit_solution(14160028943839079372)
XLA Ops:
  7.2 0.0 copy-start.6
  7.2 0.0 all-reduce.2.cloned.1.call-start
  7.2 2.8 copy.52
  10.1 0.0 copy-done.6
  10.1 0.0 copy-start.1
  10.1 0.1 fusion.40
  10.3 4.4 copy.48
  14.7 3.9 copy.49
  18.6 10.4 %fusion.47 = (f32[20,384]{1,0:T(8,128)S(1)}, f32[20,384,384]{1,2,0:T(8,128)}) fusion(pred[384,384]{0,1:T(8,128)(4,1)S(1)} %fusion.40, bf16[384,20,128]{0,2,1:T(8,128)(2,1)} %bitcast.58, bf16[384,20,128]{0,2,1:T(8,128)(2,1)} %bitcast.60), kind=kOutput, calls=%fused_computation.48 | convolution fusion | flops 766771584 | bytes 15906816 | tf_op jit(solution)/shard_map/sub | solution.py:45
  29.0 0.0 copy-done.1
  29.0 7.1 %fusion.26 = bf16[20,384,128]{1,2,0:T(8,128)(2,1)} fusion(bf16[384,20,128]{0,2,1:T(8,128)(2,1)S(1)} %bitcast.51, f32[20,384,384]{1,2,0:T(8,128)} %get-tuple-element.33, f32[20,384]{1,0:T(8,128)S(1)} %get-tuple-element.32), kind=kOutput, calls=%fused_computation.32 | convolution fusion | flops 761856000 | bytes 15759360 | tf_op jit(solution)/shard_map/shqk,skhd->sqhd/dot_general | solution.py:48
  36.1 17.8 %fusion.48 = f32[384,5120]{1,0:T(8,128)} fusion(bf16[384,2560]{0,1:T(8,128)(2,1)} %bitcast.56, bf16[5120,2560]{1,0:T(8,128)(2,1)} %param.14), kind=kOutput, calls=%fused_computation.49 | convolution fusion | flops 10066329600 | bytes 36044800 | tf_op jit(solution)/shard_map/dot_general | solution.py:52
  53.9 0.0 all-reduce.2.cloned.1.call-update
  54.0 0.2 all-gather.5.cloned.1.call-start
  54.2 0.0 copy-start.5
  54.2 189.9 %all-reduce.2.cloned.1.call-done = f32[384,5120]{1,0:T(8,128)} async-done(((f32[384,5120]{1,0:T(8,128)}), f32[384,5120]{1,0:T(8,128)}) %all-reduce.2.cloned.1.call-update) | async-done | bytes 7864336 | tf_op jit(solution)/shard_map/psum | solution.py:54
  244.1 3.4 fusion.19
  247.5 0.0 copy-start
  247.5 4.9 psum.22
  252.5 0.0 copy-done.5
  252.5 3.1 fusion.18
  255.5 4.9 psum.23
  260.5 5.0 fusion.21
  265.4 0.0 copy-done
  265.4 0.0 all-gather.5.cloned.1.call-update
  265.5 0.0 all-gather.7.cloned.1.call-start
  265.5 0.7 all-gather.7.cloned.1.call-update
  266.2 53.2 %all-gather.5.cloned.1.call-done = bf16[384,5120]{1,0:T(8,128)(2,1)} async-done(((bf16[384,2560]{1,0:T(8,128)(2,1)}), bf16[384,5120]{1,0:T(8,128)(2,1)}) %all-gather.5.cloned.1.call-update) | async-done | bytes 3932176 | tf_op jit(solution)/shard_map/all_gather | solution.py:72
  319.4 6.3 %copy.60 = bf16[384,5120]{0,1:T(8,128)(2,1)} copy(bf16[384,5120]{1,0:T(8,128)(2,1)} %all-gather.5.cloned.1.call-done) | data formatting | bytes 7864320 | tf_op jit(solution)/shard_map/all_gather | solution.py:72
  325.7 5.7 all-to-all-start
  331.3 143.7 %all-gather.1 = f32[16,1,2560]{2,1,0:T(1,128)S(1)} all-gather(f32[1,1,2560]{2,1,0:T(1,128)S(1)} %reshape.177), channel_id=2, replica_groups=mesh['dp'=16,'tensor'=2] {'dp'}, dimensions={0}, use_global_device_ids=true | all-gather | bytes 174080 | tf_op jit(solution)/shard_map/all_gather | solution.py:70
  475.0 0.7 reduce_sum.59
  475.7 17.3 %convolution_convert_fusion = bf16[384,2560]{1,0:T(8,128)(2,1)} fusion(bf16[384,5120]{1,0:T(8,128)(2,1)} %all-gather.5.cloned.1.call-done, bf16[5120,2560]{1,0:T(8,128)(2,1)} %param.14), kind=kOutput, calls=%fused_computation.20 | convolution fusion | flops 10067312640 | bytes 32112640 | tf_op jit(solution)/shard_map/dot_general | solution.py:73
  493.1 0.0 copy-start.2
  493.1 4.2 copy.54
  497.3 0.0 copy-done.2
  497.3 7.6 %fusion.49 = f32[20,384,384]{1,2,0:T(8,128)} fusion(bf16[384,20,128]{0,2,1:T(8,128)(2,1)} %bitcast.53, bf16[384,20,128]{0,2,1:T(8,128)(2,1)S(1)} %bitcast.52), kind=kOutput, calls=%fused_computation.50 | convolution fusion | flops 754974720 | bytes 15728640 | tf_op jit(solution)/shard_map/sqhd,skhd->shqk/dot_general | solution.py:88
  504.9 20.3 %fusion.32 = bf16[20,384,128]{1,2,0:T(8,128)(2,1)} fusion(bf16[384,20,128]{0,2,1:T(8,128)(2,1)} %bitcast.61, f32[20,384,384]{1,2,0:T(8,128)} %fusion.49, f32[20,384,384]{1,2,0:T(8,128)} %get-tuple-element.33, f32[20,384]{1,0:T(8,128)S(1)} %get-tuple-element.32), kind=kOutput, calls=%fused_computation.34 | convolution fusion | flops 776609664 | bytes 27555840 | tf_op jit(solution)/shard_map/shqk,skhd->sqhd/dot_general | solution.py:93
  525.2 0.0 copy-start.4
  525.2 4.1 copy.62
  529.3 0.0 copy-done.4
  529.3 19.7 %fusion.35 = bf16[20,384,128]{1,2,0:T(8,128)(2,1)} fusion(bf16[384,20,128]{0,2,1:T(8,128)(2,1)S(1)} %bitcast.59, f32[20,384,384]{1,2,0:T(8,128)} %fusion.49, f32[20,384,384]{1,2,0:T(8,128)} %get-tuple-element.33, f32[20,384]{1,0:T(8,128)S(1)} %get-tuple-element.32), kind=kOutput, calls=%fused_computation.35 | convolution fusion | flops 776609664 | bytes 27555840 | tf_op jit(solution)/shard_map/shqk,sqhd->skhd/dot_general | solution.py:96
  549.1 0.0 copy-start.3
  549.1 4.1 copy.63
  553.2 0.0 copy-done.3
  553.2 7.5 %fusion.29 = bf16[20,128,384]{2,1,0:T(8,128)(2,1)} fusion(bf16[384,20,128]{0,2,1:T(8,128)(2,1)S(1)} %bitcast.54, f32[20,384,384]{1,2,0:T(8,128)} %get-tuple-element.33, f32[20,384]{1,0:T(8,128)S(1)} %get-tuple-element.32), kind=kOutput, calls=%fused_computation.33 | convolution fusion | flops 761856000 | bytes 15759360 | tf_op jit(solution)/shard_map/shqk,sqhd->skhd/dot_general | solution.py:85
  560.7 4.0 copy.64
  564.7 0.0 all-to-all-done
  564.7 4.7 copy.73
  569.4 0.0 all-gather.7.cloned.1.call-done
  569.4 17.7 %fusion.50 = f32[320,2560]{1,0:T(8,128)} fusion(bf16[6144,320]{0,1:T(8,128)(2,1)} %bitcast.55, bf16[6144,2560]{0,1:T(8,128)(2,1)} %all-gather.7.cloned.1.call-done), kind=kOutput, calls=%fused_computation.51 | convolution fusion | flops 10066329600 | bytes 38666240 | tf_op jit(solution)/shard_map/dot_general | solution.py:78
  (4 shorter events, 0.1 us)
Async XLA Ops:
  7.2 2.9 copy-start.6
  7.2 236.9 %all-reduce.2.cloned.1.call-start = ((), (), s32[]{:S(2)}) async-start(), calls=%async_computation.1 | async-start | bytes 15728640 | tf_op jit(solution)/shard_map/psum | solution.py:54
  10.1 18.9 %copy-start.1 = (bf16[384,2560]{0,1:T(8,128)(2,1)}, bf16[384,2560]{0,1:T(8,128)(2,1)S(1)}, u32[]{:S(2)}) copy-start(bf16[384,2560]{0,1:T(8,128)(2,1)S(1)} %copy.52) | copy-start | bytes 5898244
  54.0 265.4 %all-gather.5.cloned.1.call-start = ((), (), s32[]{:S(2)}) async-start(), calls=%async_computation.2 | async-start | bytes 5898240 | tf_op jit(solution)/shard_map/all_gather | solution.py:72
  54.2 198.3 %copy-start.5 = (f32[2560]{0:T(1024)S(1)}, f32[2560]{0:T(1024)}, u32[]{:S(2)}) copy-start(f32[2560]{0:T(1024)} %param.15) | copy-start | bytes 30724
  247.5 17.9 %copy-start = (bf16[384,2560]{1,0:T(8,128)(2,1)}, bf16[384,2560]{1,0:T(8,128)(2,1)S(1)}, u32[]{:S(2)}) copy-start(bf16[384,2560]{1,0:T(8,128)(2,1)S(1)} %get-tuple-element.31) | copy-start | bytes 5898244
  265.5 303.9 %all-gather.7.cloned.1.call-start = ((), (), s32[]{:S(2)}) async-start(), calls=%async_computation.3 | async-start | bytes 33423360 | tf_op jit(solution)/shard_map/all_gather | solution.py:80
  325.7 239.1 %all-to-all-start = ((bf16[384,16,320]{0,2,1:T(8,128)(2,1)}), bf16[384,16,320]{0,2,1:T(8,128)(2,1)}, u32[]{:S(2)}, u32[]{:S(2)}) async-start(bf16[384,16,320]{0,2,1:T(8,128)(2,1)} %bitcast.50), calls=%async_computation | async-start | bytes 7864320 | tf_op jit(solution)/shard_map/all_to_all | solution.py:77
  493.1 4.2 copy-start.2
  525.2 4.1 copy-start.4
  549.1 4.1 copy-start.3
Sparse Core Ops, SparseCore 0:
  54.1 189.9 all-reduce.1
  265.6 53.7 all-gather.4
  321.5 231.1 all-gather.6
